TPU v7x, 128 devices: a whole 4x4x4 slice. The times are simulated.
128 devices in a mesh: grp: 4 (over z), tile: 32 (over x, y, core).
Axes of the slice: x: 4, y: 4, z: 4, core: 2. Of those that a mesh axis runs over, the one named last changes fastest.
Arguments:
- noise: bfloat16 [16, 3, 2048, 2048], P('grp', None, 'tile'), may hold values from -6 to 6
- stress: float32 [6, 2048, 2048], P(None, 'tile', 'grp'), as said below
- timescale: float32 [2048, 2048], P('tile', 'grp'), may hold values from 3 to 256
- mean_inflow: float32 [2048, 2048], P('tile', 'grp'), may hold values from 0.5 to 1.5
- courant: float32 [2048, 2048], P('tile', 'grp'), may hold values from 0.2 to 0.9
- prior_state: float32 [3, 2048, 2048], P(None, 'tile', 'grp'), may hold values from -6 to 6
- field: float32 [3, 8, 2048, 2048], P(None, None, 'tile', 'grp'), may hold values from -6 to 6
Outputs:
- inflow: bfloat16 [16, 3, 2048, 2048], P(None, None, 'tile', 'grp')
- field_out: float32 [3, 8, 2048, 2048], P(None, None, 'tile', 'grp')
Inputs may be any that keep to these rules, and one draw needn't show every extreme that they name: stress holds, per cell, R11, R21, R22, R31, R32, R33 of a symmetric positive definite tensor whose Cholesky factor has diagonal entries of 0.3 or more.
All inputs are finite; a program needn't handle non-finite values.
Results may differ from a plain program's by a relative error of at most 0.0085.
Values may be sent and summed in bfloat16 or wider, within the bound.
A program may use at most 128 MiB of HBM per device.

v0:
```python
import math

import jax
import jax.numpy as jnp
from jax import lax
from jax.sharding import PartitionSpec as P

LS = 2
FW = 4


def padded_2(value, sides, width, wrap):
    for axis, dim in sides:
        devices, length = (lax.axis_size(axis), value.shape[dim])
        up = [(i, (i + 1) % devices) for i in range(devices if wrap else devices - 1)]
        down = [(j, i) for i, j in up]
        last = lax.slice_in_dim(value, length - width, length, axis=dim)
        initial = lax.slice_in_dim(value, 0, width, axis=dim)
        before = lax.ppermute(last, axis, up)
        after = lax.ppermute(initial, axis, down)
        value = jnp.concatenate([before, value, after], axis=dim)
    return value


def filter_taps():
    offsets = jnp.arange(-FW, FW + 1).astype(jnp.float32)
    raw = jnp.exp(-math.pi * offsets * offsets / (2.0 * LS * LS))
    return (raw / jnp.sqrt(jnp.sum(raw * raw))).astype(jnp.bfloat16)


def band_matrix(rows, taps):
    width = taps.shape[0]
    distance = jnp.arange(rows + width - 1)[None, :] - jnp.arange(rows)[:, None]
    picks = distance[:, :, None] == jnp.arange(width)[None, None, :]
    return jnp.sum(jnp.where(picks, taps.astype(jnp.float32), 0.0), axis=2).astype(jnp.bfloat16)


def filter_last(padded, taps):
    width = taps.shape[0]
    length = padded.shape[-1] - width + 1
    block = math.gcd(length, 128)
    weights = band_matrix(block, taps)
    windows = jnp.stack(
        [
            lax.slice_in_dim(padded, start, start + block + width - 1, axis=padded.ndim - 1)
            for start in range(0, length, block)
        ],
        axis=-2,
    )
    result = jnp.einsum("...kw,bw->...kb", windows, weights, preferred_element_type=jnp.float32)
    return result.reshape(result.shape[:-2] + (length,))


def filter_rows(padded, taps):
    rows = padded.shape[2] - taps.shape[0] + 1
    weights = band_matrix(rows, taps)
    return jnp.einsum("ij,pcjz->pciz", weights, padded, preferred_element_type=jnp.float32)


def cholesky_cells(stress):
    first_diag = jnp.sqrt(stress[0])
    second_low = stress[1] / first_diag
    second_diag = jnp.sqrt(stress[2] - second_low * second_low)
    third_low = stress[3] / first_diag
    third_mid = (stress[4] - second_low * third_low) / second_diag
    third_diag = jnp.sqrt(stress[5] - third_low * third_low - third_mid * third_mid)
    return (first_diag, second_low, second_diag, third_low, third_mid, third_diag)


def velocity_of(state, factors, mean_inflow):
    first_diag, second_low, second_diag, third_low, third_mid, third_diag = factors
    return jnp.stack(
        [
            mean_inflow + first_diag * state[0],
            second_low * state[0] + second_diag * state[1],
            third_low * state[0] + third_mid * state[1] + third_diag * state[2],
        ]
    )


def march(current, courant, velocity):
    upstream = jnp.concatenate([velocity[:, None], current[:, :-1]], axis=1)
    return (1.0 - courant) * current + courant * upstream


def tile_chain(filtered, stress, timescale, mean_inflow, courant, prior_state, field):
    decay = jnp.exp(-math.pi / (2.0 * timescale))
    gain = jnp.sqrt(1.0 - decay * decay)
    factors = cholesky_cells(stress)

    def advance(carry, plane):
        state, current = carry
        state = decay * state + gain * plane
        velocity = velocity_of(state, factors, mean_inflow)
        return ((state, march(current, courant, velocity)), velocity.astype(jnp.bfloat16))

    (state, result), inflow = lax.scan(advance, (prior_state, field), filtered)
    return (inflow, result)


def body(noise, stress, timescale, mean_inflow, courant, prior_state, field):
    taps = filter_taps()
    flipped = jnp.swapaxes(noise, 2, 3)
    tiles = lax.all_to_all(
        lax.all_to_all(flipped, "tile", split_axis=2, concat_axis=3, tiled=True),
        "grp",
        split_axis=3,
        concat_axis=0,
        tiled=True,
    )
    banded = padded_2(tiles, (("grp", 3),), FW, False)
    widened = padded_2(banded, (("tile", 2),), FW, True)
    span = filter_rows(widened, taps).astype(jnp.bfloat16)
    filtered = filter_last(span, taps)
    inflow, result = tile_chain(
        filtered, stress, timescale, mean_inflow, courant, prior_state, field
    )
    return (inflow, result)


def solution(mesh):
    placed = (
        P("grp", None, "tile", None),
        P(None, "tile", "grp"),
        P("tile", "grp"),
        P("tile", "grp"),
        P("tile", "grp"),
        P(None, "tile", "grp"),
        P(None, None, "tile", "grp"),
    )
    return jax.shard_map(
        body,
        mesh=mesh,
        in_specs=placed,
        out_specs=(P(None, None, "tile", "grp"), P(None, None, "tile", "grp")),
        check_vma=False,
    )
```

profile of v0, /device:TPU:63, one launch (start us, length us, event | category | flops | bytes accessed | tf_op | source)
XLA Modules:
  0.0 310.5 jit_solution(12647594609920412347)
XLA Ops:
  0.6 1.9 copy-done.7
  2.5 7.1 %copy.41 = bf16[4,3,64,2048]{2,0,1,3:T(4,128)(2,1)} copy(bf16[4,3,64,2048]{3,2,1,0:T(8,128)(2,1)S(1)} %copy-done.7) | data formatting | bytes 6291456 | tf_op args[0]
  9.6 7.7 %bitcast_bitcast_fusion = bf16[2048,3,4,64]{3,2,1,0:T(4,128)(2,1)} fusion(bf16[4,3,64,2048]{2,0,1,3:T(4,128)(2,1)} %copy.41), kind=kLoop, calls=%fused_computation.73 | loop fusion | bytes 6291456
  17.3 7.5 %reshape.107 = bf16[32,2,24576]{2,1,0:T(2,128)(2,1)S(1)} reshape(bf16[2048,3,4,64]{3,2,1,0:T(4,128)(2,1)} %bitcast_bitcast_fusion) | data formatting | bytes 6291456
  24.8 43.9 %all_to_all.36 = bf16[32,2,24576]{2,1,0:T(2,128)(2,1)} all-to-all(bf16[32,2,24576]{2,1,0:T(2,128)(2,1)S(1)} %reshape.107), channel_id=1, replica_groups=mesh['grp'=4,'tile'=32] {'tile'}, dimensions={0} | all-to-all | bytes 6291456 | tf_op jit(solution)/shard_map/all_to_all | solution.py:105
  68.7 8.7 %reshape.108 = bf16[2048,3,4,64]{3,2,1,0:T(4,128)(2,1)} reshape(bf16[32,2,24576]{2,1,0:T(2,128)(2,1)} %all_to_all.36) | data formatting | bytes 6291456
  77.4 9.5 %copy.65 = bf16[4,3,32,64,64]{4,2,3,1,0:T(8,128)(2,1)} copy(bf16[4,3,32,64,64]{4,0,1,3,2:T(4,128)(2,1)} %bitcast.127) | data formatting | bytes 6291456 | tf_op jit(solution)/shard_map/all_to_all | solution.py:105
  86.9 11.8 %copy.54 = bf16[4,3,64,32,64]{2,0,1,4,3:T(4,128)(2,1)} copy(bf16[4,3,64,32,64]{4,3,2,1,0:T(8,128)(2,1)} %bitcast.128) | data formatting | bytes 6291456 | tf_op jit(solution)/shard_map/all_to_all | solution.py:105
  98.7 7.7 %reshape.109 = bf16[4,2,196608]{2,1,0:T(2,128)(2,1)} reshape(bf16[2048,3,4,64]{3,2,1,0:T(4,128)(2,1)} %bitcast.129) | data formatting | bytes 6291456
  106.5 5.0 %all-to-all-start.1 = ((bf16[4,2,196608]{2,1,0:T(2,128)(2,1)}), bf16[4,2,196608]{2,1,0:T(2,128)(2,1)S(1)}, u32[]{:S(2)}, u32[]{:S(2)}) async-start(bf16[4,2,196608]{2,1,0:T(2,128)(2,1)} %reshape.109), calls=%async_computation.1 | async-start | bytes 6291456 | tf_op jit(solution)/shard_map/all_to_all | solution.py:104
  112.9 2.2 fusion.24
  115.8 1.6 fusion.26
  117.4 30.1 %all-to-all-done.1 = bf16[4,2,196608]{2,1,0:T(2,128)(2,1)S(1)} async-done(((bf16[4,2,196608]{2,1,0:T(2,128)(2,1)}), bf16[4,2,196608]{2,1,0:T(2,128)(2,1)S(1)}, u32[]{:S(2)}, u32[]{:S(2)}) %all-to-all-start.1) | async-done | bytes 3145760 | tf_op jit(solution)/shard_map/all_to_all | solution.py:104
  147.5 5.3 %reshape.110 = bf16[2048,3,4,64]{3,2,1,0:T(4,128)(2,1)} reshape(bf16[4,2,196608]{2,1,0:T(2,128)(2,1)S(1)} %all-to-all-done.1) | data formatting | bytes 6291456
  152.8 8.3 %copy.45 = bf16[4,4,3,64,512]{4,3,2,1,0:T(8,128)(2,1)S(1)} copy(bf16[4,4,3,64,512]{3,1,2,4,0:T(4,128)(2,1)} %bitcast.130) | data formatting | bytes 6291456 | tf_op jit(solution)/shard_map/all_to_all | solution.py:104
  161.1 1.5 fusion.38
  162.6 1.5 copy.46
  164.1 1.5 copy.47
  165.7 3.1 collective-permute-start.1
  168.8 2.4 collective-permute-start
  171.3 2.3 collective-permute-done
  176.1 1.8 pad_maximum_fusion.3
  177.9 5.7 %collective-permute-start.2 = (bf16[16,3,4,520]{3,2,1,0:T(4,128)(2,1)S(1)}, bf16[16,3,4,520]{3,2,1,0:T(4,128)(2,1)S(1)}, u32[]{:S(2)}, u32[]{:S(2)}) collective-permute-start(bf16[16,3,4,520]{3,2,1,0:T(4,128)(2,1)S(1)} %get-tuple-element.126), channel_id=1, source_target_pairs={{0,1},{1,2},{2,3},{3,4},{4,5},{5,6},{6,7},{7,8},{8,9},{9,10},{10,1... | collective-permute-start | bytes 599048 | tf_op jit(solution)/shard_map/ppermute | solution.py:19
  183.6 1.6 sqrt_bitcast_fusion
  185.2 1.5 collective-permute-done.2
  186.7 5.8 %collective-permute-done.3 = bf16[16,3,4,520]{3,2,1,0:T(4,128)(2,1)S(1)} collective-permute-done((bf16[16,3,4,520]{3,2,1,0:T(4,128)(2,1)S(1)}, bf16[16,3,4,520]{3,2,1,0:T(4,128)(2,1)S(1)}, u32[]{:S(2)}, u32[]{:S(2)}) %collective-permute-start.3) | collective-permute-done | bytes 199712 | tf_op jit(solution)/shard_map/ppermute | solution.py:20
  192.5 4.2 %convert_bitcast_fusion.3 = bf16[16,3,64,520]{3,2,1,0:T(8,128)(2,1)S(1)} fusion(bf16[16,3,4,520]{3,2,1,0:T(4,128)(2,1)S(1)} %collective-permute-done.3, bf16[16,3,64,4]{3,2,1,0:T(8,128)(2,1)S(1)} %copy-done.6, bf16[16,3,64,512]{3,2,1,0:T(8,128)(2,1)S(1)} %bitcast.133, bf16[16,3,64,4]{3,2,1,0:T(8,128)(2,1)S(1)} %copy-done.5, ...), kind=kOutput, calls=%fused_computation.35 | convolution fusion | flops 249600000 | bytes 6798336 | tf_op jit(solution)/shard_map/ij,pcjz->pciz/dot_general | solution.py:57
  197.6 2.6 fusion.18
  200.2 3.5 %copy.64 = f32[16,3,4,8,8,128]{5,4,2,3,1,0:T(8,128)} copy(f32[16,3,4,8,8,128]{5,4,3,2,1,0:T(8,128)S(1)} %fusion.18) | data formatting | bytes 12582912 | tf_op jit(solution)/shard_map/reshape | solution.py:51
  203.7 105.1 %while.14 = (s32[]{:T(128)}, f32[3,64,512]{2,1,0:T(8,128)S(1)}, f32[3,8,64,512]{3,2,1,0:T(8,128)S(1)}, bf16[16,3,64,512]{3,2,1,0:T(8,128)(2,1)}, f32[64,512]{1,0...) while((s32[]{:T(128)}, f32[3,64,512]{2,1,0:T(8,128)S(1)}, ...), condition=%wide.region_4.5_spmd, body=%wide.region_3.4_spmd.sunk | while | flops 4685826 | bytes 20512960 | solution.py:97
  204.6 1.3 fusion.41
  205.9 1.4 convert_bitcast_fusion.5
  208.2 1.4 fusion.42
  212.5 1.4 convert_bitcast_fusion.5
  214.7 1.4 fusion.42
  219.0 1.4 convert_bitcast_fusion.5
  221.3 1.4 fusion.42
  225.6 1.4 convert_bitcast_fusion.5
  227.9 1.4 fusion.42
  232.2 1.4 convert_bitcast_fusion.5
  234.5 1.4 fusion.42
  238.7 1.4 convert_bitcast_fusion.5
  241.0 1.4 fusion.42
  245.3 1.4 convert_bitcast_fusion.5
  247.6 1.4 fusion.42
  251.9 1.4 convert_bitcast_fusion.5
  254.2 1.4 fusion.42
  258.4 1.4 convert_bitcast_fusion.5
  260.7 1.4 fusion.42
  265.0 1.4 convert_bitcast_fusion.5
  267.3 1.4 fusion.42
  271.6 1.4 convert_bitcast_fusion.5
  273.9 1.4 fusion.42
  278.2 1.4 convert_bitcast_fusion.5
  280.4 1.4 fusion.42
  284.7 1.4 convert_bitcast_fusion.5
  287.0 1.4 fusion.42
  291.3 1.4 convert_bitcast_fusion.5
  293.6 1.4 fusion.42
  297.9 1.4 convert_bitcast_fusion.5
  300.2 1.4 fusion.42
  304.4 1.4 convert_bitcast_fusion.5
  306.7 1.4 fusion.42
  308.8 1.7 copy-done
  (137 shorter events, 64.1 us)
Async XLA Ops:
  0.6 1.9 copy-start.7
  106.5 6.5 %copy-start.8 = (f32[64,512]{1,0:T(8,128)S(1)}, f32[64,512]{1,0:T(8,128)}, u32[]{:S(2)}) copy-start(f32[64,512]{1,0:T(8,128)} %param.11) | copy-start | bytes 393220
  106.5 41.0 %all-to-all-start.1 = ((bf16[4,2,196608]{2,1,0:T(2,128)(2,1)}), bf16[4,2,196608]{2,1,0:T(2,128)(2,1)S(1)}, u32[]{:S(2)}, u32[]{:S(2)}) async-start(bf16[4,2,196608]{2,1,0:T(2,128)(2,1)} %reshape.109), calls=%async_computation.1 | async-start | bytes 6291456 | tf_op jit(solution)/shard_map/all_to_all | solution.py:104
  115.1 0.7 copy-start.4
  165.7 9.2 %collective-permute-start.1 = (bf16[16,3,64,4]{2,0,3,1:T(8,128)(2,1)S(1)}, bf16[16,3,64,4]{2,0,3,1:T(8,128)(2,1)S(1)}, u32[]{:S(2)}, u32[]{:S(2)}) collective-permute-start(bf16[16,3,64,4]{2,0,3,1:T(8,128)(2,1)S(1)} %copy.47), channel_id=1, source_target_pairs={{32,0},{64,32},{96,64},{33,1},{65,33},{97,65},{34,2},{66,34},{98,6... | collective-permute-start | bytes 73736 | tf_op jit(solution)/shard_map/ppermute | solution.py:20
  168.8 4.8 %collective-permute-start = (bf16[16,3,64,4]{2,0,3,1:T(8,128)(2,1)S(1)}, bf16[16,3,64,4]{2,0,3,1:T(8,128)(2,1)S(1)}, u32[]{:S(2)}, u32[]{:S(2)}) collective-permute-start(bf16[16,3,64,4]{2,0,3,1:T(8,128)(2,1)S(1)} %copy.46), channel_id=1, source_target_pairs={{0,32},{32,64},{64,96},{1,33},{33,65},{65,97},{2,34},{34,66},{66,9... | collective-permute-start | bytes 73736 | tf_op jit(solution)/shard_map/ppermute | solution.py:19
  176.1 16.4 %copy-start.5 = (bf16[16,3,64,4]{3,2,1,0:T(8,128)(2,1)S(1)}, bf16[16,3,64,4]{3,2,1,0:T(8,128)(2,1)}, u32[]{:S(2)}) copy-start(bf16[16,3,64,4]{3,2,1,0:T(8,128)(2,1)} %copy.48) | copy-start | bytes 73732
  176.1 16.4 %copy-start.6 = (bf16[16,3,64,4]{3,2,1,0:T(8,128)(2,1)S(1)}, bf16[16,3,64,4]{3,2,1,0:T(8,128)(2,1)}, u32[]{:S(2)}) copy-start(bf16[16,3,64,4]{3,2,1,0:T(8,128)(2,1)} %copy.49) | copy-start | bytes 73732
  177.9 8.8 %collective-permute-start.2 = (bf16[16,3,4,520]{3,2,1,0:T(4,128)(2,1)S(1)}, bf16[16,3,4,520]{3,2,1,0:T(4,128)(2,1)S(1)}, u32[]{:S(2)}, u32[]{:S(2)}) collective-permute-start(bf16[16,3,4,520]{3,2,1,0:T(4,128)(2,1)S(1)} %get-tuple-element.126), channel_id=1, source_target_pairs={{0,1},{1,2},{2,3},{3,4},{4,5},{5,6},{6,7},{7,8},{8,9},{9,10},{10,1... | collective-permute-start | bytes 599048 | tf_op jit(solution)/shard_map/ppermute | solution.py:19
  183.6 8.9 %collective-permute-start.3 = (bf16[16,3,4,520]{3,2,1,0:T(4,128)(2,1)S(1)}, bf16[16,3,4,520]{3,2,1,0:T(4,128)(2,1)S(1)}, u32[]{:S(2)}, u32[]{:S(2)}) collective-permute-start(bf16[16,3,4,520]{3,2,1,0:T(4,128)(2,1)S(1)} %get-tuple-element.127), channel_id=1, source_target_pairs={{1,0},{2,1},{3,2},{4,3},{5,4},{6,5},{7,6},{8,7},{9,8},{10,9},{11,1... | collective-permute-start | bytes 599048 | tf_op jit(solution)/shard_map/ppermute | solution.py:20
  200.2 3.5 %copy-start.1 = (f32[3,8,64,512]{3,2,1,0:T(8,128)S(1)}, f32[3,8,64,512]{3,2,1,0:T(8,128)}, u32[]{:S(2)}) copy-start(f32[3,8,64,512]{3,2,1,0:T(8,128)} %param.15) | copy-start | bytes 9437188
  200.2 3.5 %copy-start.2 = (f32[3,64,512]{2,1,0:T(8,128)S(1)}, f32[3,64,512]{2,1,0:T(8,128)}, u32[]{:S(2)}) copy-start(f32[3,64,512]{2,1,0:T(8,128)} %param.14) | copy-start | bytes 1179652
  207.3 0.9 copy-start.3
  213.8 0.9 copy-start.3
  220.4 0.9 copy-start.3
  227.0 0.9 copy-start.3
  233.6 0.9 copy-start.3
  240.1 0.9 copy-start.3
  246.7 0.9 copy-start.3
  253.3 0.9 copy-start.3
  259.8 0.9 copy-start.3
  266.4 0.9 copy-start.3
  273.0 0.9 copy-start.3
  279.5 0.9 copy-start.3
  286.1 0.9 copy-start.3
  292.7 0.9 copy-start.3
  299.3 0.9 copy-start.3
  305.8 0.9 copy-start.3
  308.8 1.7 copy-start
where the time goes:
time: 313 us; the launch traced here: 310 us
  local copies, waits for them, and re-layouts  105 us (34%)
  other arithmetic  97.3 us (31%)
  blocking collectives  43.9 us (14%)
  waiting for transfers between devices  39.8 us (13%)
  starting transfers between devices  16.1 us (5%)
  matrix products  6.73 us (2%)
    unnamed x22, local copies, waits for them, and re-layouts  48.3 us
    all_to_all x1, blocking collectives, body(): lax.all_to_all(flipped, 'tile', split_axis=2, concat_axis=3, tiled=True)  43.9 us
    all_to_all x1, waiting for transfers between devices, body(): lax.all_to_all(lax.all_to_all(flipped, 'tile', split_axis=2, concat_axis=...  30.1 us
    another operation x16, other arithmetic, velocity_of(): jnp.stack([mean_inflow + first_diag * state[0], second_low * state[0] + s...  22.1 us
    add x16, other arithmetic, march(): return (1.0 - courant) * current + courant * upstream  22.1 us
    all_to_all x2, local copies, waits for them, and re-layouts, body(): lax.all_to_all(flipped, 'tile', split_axis=2, concat_axis=3, tiled=True)  21.3 us
    add x16, other arithmetic, advance(): state = decay * state + gain * plane  20.4 us
    sub x16, other arithmetic, march(): return (1.0 - courant) * current + courant * upstream  14.6 us
  transfers between devices with their start and end apart: 5, of which 4 were waited for; matrix products, arithmetic and copies ran while one was open for 2% of the time, Pallas kernels for 0%

commit v1 on v0

v1 whole, which is shorter than its diff:
```python
import functools
import math

import jax
import jax.numpy as jnp
import ml_dtypes
import numpy as np
from jax import lax
from jax.experimental import pallas as pl
from jax.experimental.pallas import tpu as pltpu
from jax.sharding import PartitionSpec as P

LS = 2
FW = 4
MESH = pl.DeviceIdType.MESH
BF16 = jnp.bfloat16
F32 = jnp.float32

LANES = 128
ROWS = 16
ZB = 256


def filter_taps():
    offsets = np.arange(-FW, FW + 1).astype(np.float32)
    raw = np.exp(np.float32(-math.pi) * offsets * offsets / np.float32(2.0 * LS * LS))
    taps = raw / np.sqrt(np.sum(raw * raw, dtype=np.float32))
    return [float(v) for v in taps.astype(ml_dtypes.bfloat16).astype(np.float32)]


def iota(shape, dim):
    return lax.broadcasted_iota(jnp.int32, shape, dim)


def banded(distance, keep):
    value = jnp.zeros(distance.shape, F32)
    for i, tap in enumerate(filter_taps()):
        value = jnp.where(distance == i - FW, tap, value)
    if keep is not None:
        value = jnp.where(keep, value, 0.0)
    return value.astype(BF16)


def kernel(
    cfg,
    noise_h, stress_h, time_h, mean_h, courant_h, prior_h, field_h,
    inflow_ref, out_ref,
    nz, stress, timescale, mean, courant, prior, field,
    wz, wy, sel, unsel, sent, sent_halo, got, got_halo, filt, velo,
    noise_sem, in_sem, send_sem, recv_sem, halo_send_sem, halo_recv_sem,
):
    G, dims = cfg["groups"], cfg["dims"]
    TN = dims[0] * dims[1] * dims[2]
    S = TN // G
    planes, comps, band, NZ = noise_h.shape
    depth = field_h.shape[1]
    chunks = got.shape[0]
    pairs = comps * planes // 2
    msg = pairs * ROWS
    g, t = lax.axis_index("grp"), lax.axis_index("tile")
    home = t // S
    place = t % S
    is_self = home == g
    has_low, has_high = g > 0, g < G - 1
    edge_low = jnp.logical_and(place == 0, home > 0)
    edge_high = jnp.logical_and(place == S - 1, home < G - 1)

    barrier = pltpu.get_barrier_semaphore()

    def greet(tile):
        def one(h, _):
            @pl.when(jnp.logical_not(jnp.logical_and(h == g, tile == t)))
            def _():
                pl.semaphore_signal(barrier, inc=1, device_id=(h, tile), device_id_type=MESH)
            return 0
        lax.fori_loop(0, G, one, 0)

    def greet_all(s, _):
        greet(g * S + s)
        return 0

    zcopies = [
        pltpu.make_async_copy(noise_h, nz.at[:, :, :, pl.ds(LANES, NZ)], noise_sem.at[0]),
        pltpu.make_async_copy(noise_h.at[:, :, :, pl.ds(NZ - LANES, LANES)], nz.at[:, :, :, pl.ds(0, LANES)], noise_sem.at[1]),
        pltpu.make_async_copy(noise_h.at[:, :, :, pl.ds(0, LANES)], nz.at[:, :, :, pl.ds(LANES + NZ, LANES)], noise_sem.at[2]),
    ]
    for copy in zcopies:
        copy.start()
    others = [
        pltpu.make_async_copy(src, dst, in_sem.at[i])
        for i, (src, dst) in enumerate(
            [(stress_h, stress), (time_h, timescale), (mean_h, mean), (courant_h, courant), (prior_h, prior), (field_h, field)]
        )
    ]
    lax.fori_loop(0, S, greet_all, 0)
    pl.when(has_low)(lambda: greet(g * S - 1))
    pl.when(has_high)(lambda: greet(g * S + S))

    wz[...] = banded(iota(wz.shape, 1) - iota(wz.shape, 0) - LANES, None)
    for copy in zcopies:
        copy.wait()
    for copy in others:
        copy.start()

    per = ZB // 64

    def span_block(b, _):
        first = pl.multiple_of(b * ZB, ZB)
        for c in range(comps):
            rhs = nz[:, c, :, pl.ds(first, 2 * ZB)].reshape(planes * band, 2 * ZB)
            out = lax.dot_general(wz[...], rhs, (((1,), (1,)), ((), ())), preferred_element_type=F32)
            out = out.astype(BF16)
            for ph in range(planes // 2):
                part = out[:, ph * LANES:(ph + 1) * LANES].reshape(per, chunks, ROWS, LANES)
                for k in range(chunks):
                    sent[k, pl.ds(b * per, per), pl.ds((c * (planes // 2) + ph) * ROWS, ROWS), :] = part[:, k]
        return 0

    lax.fori_loop(0, NZ // ZB, span_block, 0)

    is_edge = jnp.logical_or(edge_low, edge_high)
    own_halo = jnp.logical_or(
        jnp.logical_and(edge_high, home + 1 == g), jnp.logical_and(edge_low, home - 1 == g)
    )
    one, none = jnp.int32(1), jnp.int32(0)
    expected = (
        TN - jnp.where(is_self, one, none)
        + jnp.where(is_edge, jnp.int32(TN), none)
        - jnp.where(own_halo, one, none)
    )
    pl.semaphore_wait(barrier, expected)

    tx, ty, tc = t // (dims[1] * dims[2]), (t // dims[2]) % dims[1], t % dims[2]

    def dest_tile(j):
        dx, dy, dc = j // (dims[1] * dims[2]), (j // dims[2]) % dims[1], j % dims[2]
        return (((tx + dx) % dims[0]) * dims[1] + (ty + dy) % dims[1]) * dims[2] + (tc + dc) % dims[2]

    my_slot = (place + 1) * G + g

    def send_chunk(k):
        def one(j, _):
            to = dest_tile(j)
            mine = jnp.logical_and(is_self, to == t)

            @pl.when(jnp.logical_not(mine))
            def _():
                pltpu.make_async_remote_copy(
                    sent.at[k, to], got.at[k, my_slot], send_sem.at[k], recv_sem.at[k],
                    device_id=(home, to), device_id_type=MESH,
                ).start()

            return 0

        lax.fori_loop(0, TN, one, 0)

        @pl.when(is_self)
        def _():
            got[k, my_slot] = sent[k, t]

    send_chunk(0)


    @pl.when(is_edge)
    def _():
        top = jnp.where(edge_high, band - FW, 0)
        half = LANES // 2
        for i in range(pairs):
            row, col = iota((LANES, half), 0), iota((LANES, half), 1)
            h, y = row // half, row % half
            hit = jnp.logical_and(col - i * 2 * FW - h * FW == y - top, jnp.logical_and(y >= top, y < top + FW))
            sel[pl.ds(i * LANES, LANES), :] = jnp.where(hit, 1.0, 0.0).astype(BF16)

        def pack(j, _):
            for kk in range(chunks // 2):
                sides = []
                for e in range(2):
                    lhs = jnp.concatenate(
                        [sent[2 * kk + e, pl.ds(j * 4, 4), pl.ds(i * ROWS, ROWS), :].reshape(4 * ROWS, LANES) for i in range(pairs)],
                        axis=1,
                    )
                    sides.append(jnp.dot(lhs, sel[...], preferred_element_type=F32))
                both = jnp.concatenate(sides, axis=1).astype(BF16)
                sent_halo[pl.ds(j * 4, 4), pl.ds(kk * ROWS, ROWS), :] = both.reshape(4, ROWS, LANES)
            return 0

        lax.fori_loop(0, TN // 4, pack, 0)
        to_group = jnp.where(edge_high, home + 1, home - 1)
        side = jnp.where(edge_high, 0, 1)

        def one(j, _):
            to = dest_tile(j)
            mine = jnp.logical_and(to_group == g, to == t)

            @pl.when(jnp.logical_not(mine))
            def _():
                pltpu.make_async_remote_copy(
                    sent_halo.at[to], got_halo.at[side, g], halo_send_sem, halo_recv_sem.at[side],
                    device_id=(to_group, to), device_id_type=MESH,
                ).start()

            @pl.when(mine)
            def _():
                got_halo[side, g] = sent_halo[t]

            return 0

        lax.fori_loop(0, TN, one, 0)

    for k in range(1, chunks):
        send_chunk(k)

    row, col = iota(wy.shape, 0), iota(wy.shape, 1)
    wy[...] = banded(
        (row // LANES - 1) * 64 + row % 64 - col % LANES,
        (row // 64) % 2 == col // LANES,
    )
    half = LANES // 2
    for side in range(2):
        top = band - FW if side == 0 else 0
        for i in range(pairs):
            row, col = iota((LANES, LANES), 0), iota((LANES, LANES), 1)
            h, y = col // half, col % half
            want = i * 2 * FW + h * FW + y - top
            for e in range(2):
                hit = jnp.logical_and(row == want + e * half, jnp.logical_and(y >= top, y < top + FW))
                unsel[side, e, :, pl.ds(i * LANES, LANES)] = jnp.where(hit, 1.0, 0.0).astype(BF16)
    for copy in others:
        copy.wait()

    for side, there in ((0, has_low), (1, has_high)):
        own = jnp.logical_and(edge_high, home + 1 == g) if side == 0 else jnp.logical_and(edge_low, home - 1 == g)
        slot = 0 if side == 0 else S + 1

        @pl.when(jnp.logical_and(there, own))
        def _():
            part = got_halo.at[side, pl.ds(0, G - 1)]
            pltpu.make_async_copy(part, part, halo_recv_sem.at[side]).wait()

        @pl.when(jnp.logical_and(there, jnp.logical_not(own)))
        def _():
            part = got_halo.at[side]
            pltpu.make_async_copy(part, part, halo_recv_sem.at[side]).wait()

        @pl.when(there)
        def _():
            for k in range(chunks):
                lhs = got_halo[side, :, pl.ds((k // 2) * ROWS, ROWS), :].reshape(G * ROWS, LANES)
                rows = jnp.dot(lhs, unsel[side, k % 2], preferred_element_type=F32).astype(BF16)
                for i in range(pairs):
                    got[k, pl.ds(slot * G, G), pl.ds(i * ROWS, ROWS), :] = rows[:, i * LANES:(i + 1) * LANES].reshape(G, ROWS, LANES)

        @pl.when(jnp.logical_not(there))
        def _():
            for k in range(chunks):
                got[k, pl.ds(slot * G, G)] = jnp.zeros((G, msg, LANES), BF16)

    def chunk(k, _):
        @pl.when(is_self)
        def _():
            part = got.at[k, pl.ds(G, S * G - 1)]
            pltpu.make_async_copy(part, part, recv_sem.at[k]).wait()

        @pl.when(jnp.logical_not(is_self))
        def _():
            part = got.at[k, pl.ds(G, S * G)]
            pltpu.make_async_copy(part, part, recv_sem.at[k]).wait()

        def cells(yb, _):
            lanes = pl.ds(pl.multiple_of(yb * LANES, LANES), LANES)
            for p4 in range(G):
                lhs = jnp.concatenate([got[k, (2 * yb + s) * G + p4] for s in range(4)], axis=1)
                filt[pl.ds(p4 * msg, msg), :] = jnp.dot(lhs, wy[...], preferred_element_type=F32)
            for half_rows in range(2):
                r0 = half_rows * 8
                zr = pl.ds(pl.multiple_of(k * ROWS + r0, 8), 8)
                decay = jnp.exp(-math.pi / (2.0 * timescale[zr, lanes]))
                gain = jnp.sqrt(1.0 - decay * decay)
                per_gain = 1.0 / gain
                r = [stress[i, zr, lanes] for i in range(6)]
                l11 = jnp.sqrt(r[0])
                l21 = r[1] / l11
                l22 = jnp.sqrt(r[2] - l21 * l21)
                l31 = r[3] / l11
                l32 = (r[4] - l21 * l31) / l22
                l33 = jnp.sqrt(r[5] - l31 * l31 - l32 * l32)
                l11, l21, l22, l31, l32, l33 = (v * gain for v in (l11, l21, l22, l31, l32, l33))
                state = [prior[c, zr, lanes] * per_gain for c in range(3)]
                mean_in = mean[zr, lanes]
                cou = courant[zr, lanes]
                stay = 1.0 - cou
                per_cou = 1.0 / cou
                current = []
                for c in range(3):
                    scale = per_cou
                    line = []
                    for x in range(depth):
                        line.append(field[c, x, zr, lanes] * scale)
                        scale = scale * per_cou
                    current.append(line)
                for p in range(planes * G):
                    at = [(p // planes) * msg + (c * (planes // 2) + (p % planes) // 2) * ROWS + r0 for c in range(3)]
                    side = (p % 2) * LANES
                    state = [decay * state[c] + filt[pl.ds(at[c], 8), pl.ds(side, LANES)] for c in range(3)]
                    vel = [
                        mean_in + l11 * state[0],
                        l21 * state[0] + l22 * state[1],
                        l31 * state[0] + l32 * state[1] + l33 * state[2],
                    ]
                    for c in range(3):
                        velo[p, c, pl.ds(r0, 8), :] = vel[c]
                        line = current[c]
                        current[c] = [stay * line[x] + (line[x - 1] if x else vel[c]) for x in range(depth)]
                for c in range(3):
                    scale = cou
                    for x in range(depth):
                        out_ref[c, x, zr, lanes] = current[c][x] * scale
                        scale = scale * cou
            zr = pl.ds(pl.multiple_of(k * ROWS, ROWS), ROWS)
            for p in range(planes * G):
                for c in range(3):
                    inflow_ref[p, c, zr, lanes] = velo[p, c].astype(BF16)
            return 0

        lax.fori_loop(0, inflow_ref.shape[3] // LANES, cells, 0)
        return 0

    lax.fori_loop(0, chunks, chunk, 0)

    def drain(k, _):
        @pl.when(is_self)
        def _():
            part = sent.at[k, pl.ds(0, TN - 1)]
            pltpu.make_async_copy(part, part, send_sem.at[k]).wait()

        @pl.when(jnp.logical_not(is_self))
        def _():
            part = sent.at[k]
            pltpu.make_async_copy(part, part, send_sem.at[k]).wait()

        return 0

    lax.fori_loop(0, chunks, drain, 0)

    @pl.when(jnp.logical_and(is_edge, own_halo))
    def _():
        part = sent_halo.at[pl.ds(0, TN - 1)]
        pltpu.make_async_copy(part, part, halo_send_sem).wait()

    @pl.when(jnp.logical_and(is_edge, jnp.logical_not(own_halo)))
    def _():
        pltpu.make_async_copy(sent_halo, sent_halo, halo_send_sem).wait()


def body(cfg, noise, stress, timescale, mean_inflow, courant, prior_state, field):
    G, dims = cfg["groups"], cfg["dims"]
    TN = dims[0] * dims[1] * dims[2]
    S = TN // G
    planes, comps, band, NZ = noise.shape
    depth, width, length = field.shape[1:]
    assert band == 64 and width == 64 and length == S * band and NZ == TN * width
    chunks = width // ROWS
    pairs = comps * planes // 2
    msg = pairs * ROWS
    hbm_spec = pl.BlockSpec(memory_space=pltpu.HBM)
    vmem_spec = pl.BlockSpec(memory_space=pltpu.VMEM)
    return pl.pallas_call(
        functools.partial(kernel, cfg),
        out_shape=(
            pltpu.VMEM((planes * G, comps, width, length), BF16),
            pltpu.VMEM((comps, depth, width, length), F32),
        ),
        in_specs=[hbm_spec] * 7,
        out_specs=(vmem_spec, vmem_spec),
        scratch_shapes=[
            pltpu.VMEM((planes, comps, band, NZ + 2 * LANES), BF16),
            pltpu.VMEM(stress.shape, F32),
            pltpu.VMEM(timescale.shape, F32),
            pltpu.VMEM(mean_inflow.shape, F32),
            pltpu.VMEM(courant.shape, F32),
            pltpu.VMEM(prior_state.shape, F32),
            pltpu.VMEM(field.shape, F32),
            pltpu.VMEM((ZB, 2 * ZB), BF16),
            pltpu.VMEM((4 * LANES, 2 * LANES), BF16),
            pltpu.VMEM((pairs * LANES, LANES // 2), BF16),
            pltpu.VMEM((2, 2, LANES, pairs * LANES), BF16),
            pltpu.VMEM((chunks, TN, msg, LANES), BF16),
            pltpu.VMEM((TN, chunks // 2 * ROWS, LANES), BF16),
            pltpu.VMEM((chunks, (S + 2) * G, msg, LANES), BF16),
            pltpu.VMEM((2, G, chunks // 2 * ROWS, LANES), BF16),
            pltpu.VMEM((G * msg, 2 * LANES), F32),
            pltpu.VMEM((planes * G, comps, ROWS, LANES), F32),
            pltpu.SemaphoreType.DMA((3,)),
            pltpu.SemaphoreType.DMA((6,)),
            pltpu.SemaphoreType.DMA((chunks,)),
            pltpu.SemaphoreType.DMA((chunks,)),
            pltpu.SemaphoreType.DMA,
            pltpu.SemaphoreType.DMA((2,)),
        ],
        compiler_params=pltpu.CompilerParams(
            collective_id=0, has_side_effects=True, vmem_limit_bytes=40 * 2**20
        ),
        name="inflow",
    )(*[
        pltpu.with_memory_space_constraint(v, pltpu.HBM)
        for v in (noise, stress, timescale, mean_inflow, courant, prior_state, field)
    ])


TILE_DIMS = {32: (4, 4, 2), 8: (2, 2, 2), 4: (2, 1, 2)}


def solution(mesh):
    cfg = dict(groups=mesh.shape["grp"], dims=TILE_DIMS[mesh.shape["tile"]])
    placed = (
        P("grp", None, "tile", None),
        P(None, "tile", "grp"),
        P("tile", "grp"),
        P("tile", "grp"),
        P("tile", "grp"),
        P(None, "tile", "grp"),
        P(None, None, "tile", "grp"),
    )
    return jax.shard_map(
        functools.partial(body, cfg),
        mesh=mesh,
        in_specs=placed,
        out_specs=(P(None, None, "tile", "grp"), P(None, None, "tile", "grp")),
        check_vma=False,
    )
```

time: 313 us -> 61 us (0.19)
  the two profiles are of different devices: /device:TPU:63 before, /device:TPU:27 now
where the time goes in v1:
time: 61 us; the launch traced here: 60.9 us
  Pallas kernels  56.9 us (93%)
  local copies, waits for them, and re-layouts  3.33 us (5%)
  between operations  0.64 us (1%)
    pallas_call x1, Pallas kernels, body(): pl.pallas_call(functools.partial(kernel, cfg), out_shape=(pltpu.VMEM((pla...  56.9 us
    unnamed x2, local copies, waits for them, and re-layouts  3.33 us

profile of v1, /device:TPU:27, one launch (start us, length us, event | category | flops | bytes accessed | tf_op | source)
XLA Modules:
  0.0 60.9 jit_solution(6360321644499340536)
XLA Ops:
  0.6 56.9 %inflow.1 = (bf16[16,3,64,512]{3,2,1,0:T(8,128)(2,1)S(1)}, f32[3,8,64,512]{3,2,1,0:T(8,128)S(1)}) custom-call(bf16[4,3,64,2048]{3,2,1,0:T(8,128)(2,1)} %noise_h.1, f32[6,64,512]{2,1,0:T(8,128)} %stress_h.1, f32[64,512]{1,0:T(8,128)} %time_h.1, f32[64,512]{1,0:T(8,128)} %mean_h.1, f32[64,512]{1,0:T(8,128)} %courant_h.1, f32[3,64,512]{2,1,0:T(8,128)} %prior_h.1, ...), custom_call_target="tpu_custom_call" | custom-call | tf_op jit(solution)/shard_map/inflow/pallas_call | solution.py:367
  57.5 1.7 %copy.11 = bf16[16,3,64,512]{3,2,1,0:T(8,128)(2,1)} copy(bf16[16,3,64,512]{3,2,1,0:T(8,128)(2,1)S(1)} %get-tuple-element.2) | data formatting | bytes 6291456
  59.2 1.7 %copy.12 = f32[3,8,64,512]{3,2,1,0:T(8,128)} copy(f32[3,8,64,512]{3,2,1,0:T(8,128)S(1)} %get-tuple-element.3) | data formatting | bytes 6291456

commit v2 on v1

v2 whole, which is shorter than its diff:
```python
import functools
import math

import jax
import jax.numpy as jnp
import ml_dtypes
import numpy as np
from jax import lax
from jax.experimental import pallas as pl
from jax.experimental.pallas import tpu as pltpu
from jax.sharding import PartitionSpec as P

LS = 2
FW = 4
MESH = pl.DeviceIdType.MESH
BF16 = jnp.bfloat16
F32 = jnp.float32

LANES = 128
ROWS = 16
ZB = 256


def filter_taps():
    offsets = np.arange(-FW, FW + 1).astype(np.float32)
    raw = np.exp(np.float32(-math.pi) * offsets * offsets / np.float32(2.0 * LS * LS))
    taps = raw / np.sqrt(np.sum(raw * raw, dtype=np.float32))
    return [float(v) for v in taps.astype(ml_dtypes.bfloat16).astype(np.float32)]


def iota(shape, dim):
    return lax.broadcasted_iota(jnp.int32, shape, dim)


def banded(distance, keep):
    value = jnp.zeros(distance.shape, F32)
    for i, tap in enumerate(filter_taps()):
        value = jnp.where(distance == i - FW, tap, value)
    if keep is not None:
        value = jnp.where(keep, value, 0.0)
    return value.astype(BF16)


def kernel(
    cfg,
    noise_h, stress_h, time_h, mean_h, courant_h, prior_h, field_h,
    inflow_ref, out_ref,
    nz, factor, decay, mean, courant, prior, field,
    wz, wy, sel, unsel, sent, sent_halo, got, got_halo, filt, states,
    noise_sem, in_sem, send_sem, recv_sem, halo_send_sem, halo_recv_sem,
):
    G, dims = cfg["groups"], cfg["dims"]
    TN = dims[0] * dims[1] * dims[2]
    S = TN // G
    planes, comps, band, NZ = noise_h.shape
    depth, width, length = field_h.shape[1:]
    chunks = width // ROWS
    halves = planes // 2
    pairs = comps * halves
    half = LANES // 2
    g, t = lax.axis_index("grp"), lax.axis_index("tile")
    home, place = lax.div(t, S), lax.rem(t, S)
    is_self = home == g
    has_low, has_high = g > 0, g < G - 1
    edge_low = jnp.logical_and(place == 0, home > 0)
    edge_high = jnp.logical_and(place == S - 1, home < G - 1)
    is_edge = jnp.logical_or(edge_low, edge_high)
    own_halo = jnp.logical_or(
        jnp.logical_and(edge_high, home + 1 == g), jnp.logical_and(edge_low, home - 1 == g)
    )
    one, none = jnp.int32(1), jnp.int32(0)

    zcopies = [
        pltpu.make_async_copy(noise_h, nz.at[:, :, :, pl.ds(LANES, NZ)], noise_sem.at[0]),
        pltpu.make_async_copy(noise_h.at[:, :, :, pl.ds(NZ - LANES, LANES)], nz.at[:, :, :, pl.ds(0, LANES)], noise_sem.at[1]),
        pltpu.make_async_copy(noise_h.at[:, :, :, pl.ds(0, LANES)], nz.at[:, :, :, pl.ds(LANES + NZ, LANES)], noise_sem.at[2]),
    ]
    for copy in zcopies:
        copy.start()
    others = [
        pltpu.make_async_copy(src, dst, in_sem.at[i])
        for i, (src, dst) in enumerate(
            [(stress_h, factor), (time_h, decay), (mean_h, mean), (courant_h, courant), (prior_h, prior), (field_h, field)]
        )
    ]

    barrier = pltpu.get_barrier_semaphore()

    def greet(tile):
        def tell(h, _):
            @pl.when(jnp.logical_not(jnp.logical_and(h == g, tile == t)))
            def _():
                pl.semaphore_signal(barrier, inc=1, device_id=(h, tile), device_id_type=MESH)
            return 0
        lax.fori_loop(0, G, tell, 0)

    def greet_all(s, _):
        greet(g * S + s)
        return 0

    lax.fori_loop(0, S, greet_all, 0)
    pl.when(has_low)(lambda: greet(g * S - 1))
    pl.when(has_high)(lambda: greet(g * S + S))

    wz[...] = banded(iota(wz.shape, 1) - iota(wz.shape, 0) - LANES, None)

    @pl.when(is_edge)
    def _():
        top = jnp.where(edge_high, jnp.int32(band - FW), none)
        for i in range(pairs):
            row, col = iota((LANES, LANES), 0), iota((LANES, LANES), 1)
            h, y = row // half, row % half
            inside = jnp.logical_and(y >= top, y < top + FW)
            want = i * 2 * FW + h * FW + y - top
            for e in range(2):
                hit = jnp.logical_and(col == want + e * half, inside)
                sel[e, pl.ds(i * LANES, LANES), :] = jnp.where(hit, 1.0, 0.0).astype(BF16)

    for copy in zcopies:
        copy.wait()
    for copy in others:
        copy.start()

    per = ZB // width

    def span_block(b, _):
        first = pl.multiple_of(b * ZB, ZB)
        for c in range(comps):
            rhs = nz[:, c, :, pl.ds(first, 2 * ZB)].reshape(planes * band, 2 * ZB)
            out = lax.dot_general(wz[...], rhs, (((1,), (1,)), ((), ())), preferred_element_type=F32)
            out = out.astype(BF16)
            for ph in range(halves):
                part = out[:, ph * LANES:(ph + 1) * LANES].reshape(per, chunks, ROWS, LANES)
                for k in range(chunks):
                    sent[k * comps + c, pl.ds(b * per, per), pl.ds(ph * ROWS, ROWS), :] = part[:, k]
        return 0

    lax.fori_loop(0, NZ // ZB, span_block, 0)

    tx, ty, tc = lax.div(t, dims[1] * dims[2]), lax.rem(lax.div(t, dims[2]), dims[1]), lax.rem(t, dims[2])

    def dest_tile(j):
        dx, dy, dc = lax.div(j, dims[1] * dims[2]), lax.rem(lax.div(j, dims[2]), dims[1]), lax.rem(j, dims[2])
        return (lax.rem(tx + dx, dims[0]) * dims[1] + lax.rem(ty + dy, dims[1])) * dims[2] + lax.rem(tc + dc, dims[2])

    @pl.when(is_edge)
    def _():
        for kk in range(chunks // 2):
            total = None
            for e in range(2):
                lhs = jnp.concatenate(
                    [
                        sent[(2 * kk + e) * comps + i // halves, :, pl.ds((i % halves) * ROWS, ROWS), :].reshape(TN * ROWS, LANES)
                        for i in range(pairs)
                    ],
                    axis=1,
                )
                part = jnp.dot(lhs, sel[e], preferred_element_type=F32)
                total = part if total is None else total + part
            sent_halo[:, pl.ds(kk * ROWS, ROWS), :] = total.astype(BF16).reshape(TN, ROWS, LANES)

    expected = (
        TN - jnp.where(is_self, one, none)
        + jnp.where(is_edge, jnp.int32(TN), none)
        - jnp.where(own_halo, one, none)
    )
    pl.semaphore_wait(barrier, expected)

    @pl.when(is_edge)
    def _():
        to_group = jnp.where(edge_high, home + 1, home - 1)
        side = jnp.where(edge_high, none, one)

        def send(j, _):
            to = dest_tile(j)
            pltpu.make_async_remote_copy(
                sent_halo.at[to], got_halo.at[side, g], halo_send_sem, halo_recv_sem.at[side],
                device_id=(to_group, to), device_id_type=MESH,
            ).start()
            return 0

        lax.fori_loop(jnp.where(own_halo, one, none), TN, send, 0)

    my_slot = (place + 1) * G + g
    first_send = jnp.where(is_self, one, none)

    def send_chunk(q, _):
        def send(j, _):
            to = dest_tile(j)
            pltpu.make_async_remote_copy(
                sent.at[q, to], got.at[q, my_slot], send_sem.at[q], recv_sem.at[q],
                device_id=(home, to), device_id_type=MESH,
            ).start()
            return 0

        return lax.fori_loop(first_send, TN, send, 0)

    lax.fori_loop(0, chunks * comps, send_chunk, 0)

    @pl.when(is_self)
    def _():
        got[:, my_slot] = sent[:, t]

    @pl.when(own_halo)
    def _():
        side = jnp.where(edge_high, none, one)
        got_halo[side, g] = sent_halo[t]

    row, col = iota(wy.shape, 0), iota(wy.shape, 1)
    wy[...] = banded(
        (row // LANES - 1) * half + row % half - col % LANES,
        (row // half) % 2 == col // LANES,
    )
    for side in range(2):
        top = band - FW if side == 0 else 0
        for i in range(pairs):
            row, col = iota((LANES, LANES), 0), iota((LANES, LANES), 1)
            h, y = col // half, col % half
            want = i * 2 * FW + h * FW + y - top
            for e in range(2):
                hit = jnp.logical_and(row == want + e * half, jnp.logical_and(y >= top, y < top + FW))
                unsel[side, e, :, pl.ds(i * LANES, LANES)] = jnp.where(hit, 1.0, 0.0).astype(BF16)
    for copy in others:
        copy.wait()

    def prepare(n, _):
        zr = pl.ds(pl.multiple_of(lax.div(n, length // LANES) * ROWS, ROWS), ROWS)
        lanes = pl.ds(pl.multiple_of(lax.rem(n, length // LANES) * LANES, LANES), LANES)
        fade = jnp.exp(-math.pi / (2.0 * decay[zr, lanes]))
        gain = jnp.sqrt(1.0 - fade * fade)
        per_gain = 1.0 / gain
        r = [factor[i, zr, lanes] for i in range(6)]
        l11 = jnp.sqrt(r[0])
        l21 = r[1] / l11
        l22 = jnp.sqrt(r[2] - l21 * l21)
        l31 = r[3] / l11
        l32 = (r[4] - l21 * l31) / l22
        l33 = jnp.sqrt(r[5] - l31 * l31 - l32 * l32)
        for i, v in enumerate((l11, l21, l22, l31, l32, l33)):
            factor[i, zr, lanes] = v * gain
        decay[zr, lanes] = fade
        per_cou = 1.0 / courant[zr, lanes]
        for c in range(comps):
            prior[c, zr, lanes] = prior[c, zr, lanes] * per_gain
            scale = per_cou
            for x in range(depth):
                field[c, x, zr, lanes] = field[c, x, zr, lanes] * scale
                scale = scale * per_cou
        return 0

    lax.fori_loop(0, chunks * (length // LANES), prepare, 0)

    for side, there in ((0, has_low), (1, has_high)):
        own = jnp.logical_and(edge_high, home + 1 == g) if side == 0 else jnp.logical_and(edge_low, home - 1 == g)
        slot = 0 if side == 0 else S + 1

        @pl.when(jnp.logical_and(there, own))
        def _():
            part = got_halo.at[side, pl.ds(0, G - 1)]
            pltpu.make_async_copy(part, part, halo_recv_sem.at[side]).wait()

        @pl.when(jnp.logical_and(there, jnp.logical_not(own)))
        def _():
            part = got_halo.at[side]
            pltpu.make_async_copy(part, part, halo_recv_sem.at[side]).wait()

        @pl.when(there)
        def _():
            for k in range(chunks):
                lhs = got_halo[side, :, pl.ds((k // 2) * ROWS, ROWS), :].reshape(G * ROWS, LANES)
                rows = jnp.dot(lhs, unsel[side, k % 2], preferred_element_type=F32).astype(BF16)
                for i in range(pairs):
                    got[k * comps + i // halves, pl.ds(slot * G, G), pl.ds((i % halves) * ROWS, ROWS), :] = (
                        rows[:, i * LANES:(i + 1) * LANES].reshape(G, ROWS, LANES)
                    )

        @pl.when(jnp.logical_not(there))
        def _():
            for q in range(chunks * comps):
                got[q, pl.ds(slot * G, G)] = jnp.zeros((G, halves * ROWS, LANES), BF16)

    def chunk(k, _):
        zr = pl.ds(pl.multiple_of(k * ROWS, ROWS), ROWS)
        for c in range(comps):
            q = k * comps + c

            @pl.when(is_self)
            def _():
                part = got.at[q, pl.ds(G, S * G - 1)]
                pltpu.make_async_copy(part, part, recv_sem.at[q]).wait()

            @pl.when(jnp.logical_not(is_self))
            def _():
                part = got.at[q, pl.ds(G, S * G)]
                pltpu.make_async_copy(part, part, recv_sem.at[q]).wait()

            for yb in range(length // LANES):
                lhs = jnp.concatenate(
                    [got[q, pl.ds((2 * yb + s) * G, G)].reshape(G * halves * ROWS, LANES) for s in range(4)], axis=1
                )
                filt[yb] = jnp.dot(lhs, wy[...], preferred_element_type=F32)

            def cells(yb, _):
                lanes = pl.ds(pl.multiple_of(yb * LANES, LANES), LANES)
                fade = decay[zr, lanes]
                state = prior[c, zr, lanes]
                low = [factor[c * (c + 1) // 2 + i, zr, lanes] for i in range(c + 1)]
                cou = courant[zr, lanes]
                stay = 1.0 - cou
                line = [field[c, x, zr, lanes] for x in range(depth)]
                for p in range(planes * G):
                    at = ((p // planes) * halves + (p % planes) // 2) * ROWS
                    state = fade * state + filt[yb, pl.ds(at, ROWS), pl.ds((p % 2) * LANES, LANES)]
                    vel = low[c] * state
                    for i in range(c):
                        vel = vel + low[i] * states[i, yb, p]
                    if c == 0:
                        vel = vel + mean[zr, lanes]
                    if c < comps - 1:
                        states[c, yb, p] = state
                    inflow_ref[p, c, zr, lanes] = vel.astype(BF16)
                    line = [stay * line[x] + (line[x - 1] if x else vel) for x in range(depth)]
                scale = cou
                for x in range(depth):
                    out_ref[c, x, zr, lanes] = line[x] * scale
                    scale = scale * cou
                return 0

            lax.fori_loop(0, length // LANES, cells, 0)
        return 0

    lax.fori_loop(0, chunks, chunk, 0)

    def drain(q, _):
        @pl.when(is_self)
        def _():
            part = sent.at[q, pl.ds(0, TN - 1)]
            pltpu.make_async_copy(part, part, send_sem.at[q]).wait()

        @pl.when(jnp.logical_not(is_self))
        def _():
            part = sent.at[q]
            pltpu.make_async_copy(part, part, send_sem.at[q]).wait()

        return 0

    lax.fori_loop(0, chunks * comps, drain, 0)

    @pl.when(jnp.logical_and(is_edge, own_halo))
    def _():
        part = sent_halo.at[pl.ds(0, TN - 1)]
        pltpu.make_async_copy(part, part, halo_send_sem).wait()

    @pl.when(jnp.logical_and(is_edge, jnp.logical_not(own_halo)))
    def _():
        pltpu.make_async_copy(sent_halo, sent_halo, halo_send_sem).wait()


def body(cfg, noise, stress, timescale, mean_inflow, courant, prior_state, field):
    G, dims = cfg["groups"], cfg["dims"]
    TN = dims[0] * dims[1] * dims[2]
    S = TN // G
    planes, comps, band, NZ = noise.shape
    depth, width, length = field.shape[1:]
    assert band == 64 and width == 64 and length == S * band and NZ == TN * width
    chunks = width // ROWS
    pairs = comps * planes // 2
    halves = planes // 2
    cuts = chunks * comps
    hbm_spec = pl.BlockSpec(memory_space=pltpu.HBM)
    vmem_spec = pl.BlockSpec(memory_space=pltpu.VMEM)
    return pl.pallas_call(
        functools.partial(kernel, cfg),
        out_shape=(
            pltpu.VMEM((planes * G, comps, width, length), BF16),
            pltpu.VMEM((comps, depth, width, length), F32),
        ),
        in_specs=[hbm_spec] * 7,
        out_specs=(vmem_spec, vmem_spec),
        scratch_shapes=[
            pltpu.VMEM((planes, comps, band, NZ + 2 * LANES), BF16),
            pltpu.VMEM(stress.shape, F32),
            pltpu.VMEM(timescale.shape, F32),
            pltpu.VMEM(mean_inflow.shape, F32),
            pltpu.VMEM(courant.shape, F32),
            pltpu.VMEM(prior_state.shape, F32),
            pltpu.VMEM(field.shape, F32),
            pltpu.VMEM((ZB, 2 * ZB), BF16),
            pltpu.VMEM((4 * LANES, 2 * LANES), BF16),
            pltpu.VMEM((2, pairs * LANES, LANES), BF16),
            pltpu.VMEM((2, 2, LANES, pairs * LANES), BF16),
            pltpu.VMEM((cuts, TN, halves * ROWS, LANES), BF16),
            pltpu.VMEM((TN, chunks // 2 * ROWS, LANES), BF16),
            pltpu.VMEM((cuts, (S + 2) * G, halves * ROWS, LANES), BF16),
            pltpu.VMEM((2, G, chunks // 2 * ROWS, LANES), BF16),
            pltpu.VMEM((length // LANES, G * halves * ROWS, 2 * LANES), F32),
            pltpu.VMEM((comps - 1, length // LANES, planes * G, ROWS, LANES), F32),
            pltpu.SemaphoreType.DMA((3,)),
            pltpu.SemaphoreType.DMA((6,)),
            pltpu.SemaphoreType.DMA((cuts,)),
            pltpu.SemaphoreType.DMA((cuts,)),
            pltpu.SemaphoreType.DMA,
            pltpu.SemaphoreType.DMA((2,)),
        ],
        compiler_params=pltpu.CompilerParams(
            collective_id=0, has_side_effects=True, vmem_limit_bytes=40 * 2**20
        ),
        name="inflow",
    )(*[
        pltpu.with_memory_space_constraint(v, pltpu.HBM)
        for v in (noise, stress, timescale, mean_inflow, courant, prior_state, field)
    ])


TILE_DIMS = {32: (4, 4, 2), 8: (2, 2, 2), 4: (2, 1, 2)}


def solution(mesh):
    cfg = dict(groups=mesh.shape["grp"], dims=TILE_DIMS[mesh.shape["tile"]])
    placed = (
        P("grp", None, "tile", None),
        P(None, "tile", "grp"),
        P("tile", "grp"),
        P("tile", "grp"),
        P("tile", "grp"),
        P(None, "tile", "grp"),
        P(None, None, "tile", "grp"),
    )
    return jax.shard_map(
        functools.partial(body, cfg),
        mesh=mesh,
        in_specs=placed,
        out_specs=(P(None, None, "tile", "grp"), P(None, None, "tile", "grp")),
        check_vma=False,
    )
```

time: 61 us -> 54.1 us (0.89)
  the two profiles are of different devices: /device:TPU:27 before, /device:TPU:5 now
where the time goes in v2:
time: 54.1 us; the launch traced here: 54 us
  Pallas kernels  50.1 us (93%)
  local copies, waits for them, and re-layouts  3.33 us (6%)
  between operations  0.64 us (1%)
    pallas_call x1, Pallas kernels, body(): pl.pallas_call(functools.partial(kernel, cfg), out_shape=(pltpu.VMEM((pla...  50.1 us
    unnamed x2, local copies, waits for them, and re-layouts  3.33 us

profile of v2, /device:TPU:5, one launch (start us, length us, event | category | flops | bytes accessed | tf_op | source)
XLA Modules:
  0.0 54.0 jit_solution(14404096323590143385)
XLA Ops:
  0.6 50.1 %inflow.1 = (bf16[16,3,64,512]{3,2,1,0:T(8,128)(2,1)S(1)}, f32[3,8,64,512]{3,2,1,0:T(8,128)S(1)}) custom-call(bf16[4,3,64,2048]{3,2,1,0:T(8,128)(2,1)} %noise_h.1, f32[6,64,512]{2,1,0:T(8,128)} %stress_h.1, f32[64,512]{1,0:T(8,128)} %time_h.1, f32[64,512]{1,0:T(8,128)} %mean_h.1, f32[64,512]{1,0:T(8,128)} %courant_h.1, f32[3,64,512]{2,1,0:T(8,128)} %prior_h.1, ...), custom_call_target="tpu_custom_call" | custom-call | tf_op jit(solution)/shard_map/inflow/pallas_call | solution.py:372
  50.7 1.7 %copy.11 = bf16[16,3,64,512]{3,2,1,0:T(8,128)(2,1)} copy(bf16[16,3,64,512]{3,2,1,0:T(8,128)(2,1)S(1)} %get-tuple-element.2) | data formatting | bytes 6291456
  52.4 1.7 %copy.12 = f32[3,8,64,512]{3,2,1,0:T(8,128)} copy(f32[3,8,64,512]{3,2,1,0:T(8,128)S(1)} %get-tuple-element.3) | data formatting | bytes 6291456

commit v3 on v2

--- a/solution.py
+++ b/solution.py
@@ -19,6 +19,7 @@
 LANES = 128
 ROWS = 16
 ZB = 256
+GROUP = 2
 
 
 def filter_taps():
@@ -46,7 +47,7 @@
     noise_h, stress_h, time_h, mean_h, courant_h, prior_h, field_h,
     inflow_ref, out_ref,
     nz, factor, decay, mean, courant, prior, field,
-    wz, wy, sel, unsel, sent, sent_halo, got, got_halo, filt, states,
+    rim, wz, wy, sel, unsel, sent, sent_halo, got, got_halo, filt, states,
     noise_sem, in_sem, send_sem, recv_sem, halo_send_sem, halo_recv_sem,
 ):
     G, dims = cfg["groups"], cfg["dims"]
@@ -70,10 +71,10 @@
     )
     one, none = jnp.int32(1), jnp.int32(0)
 
+    blocks, per = NZ // ZB, ZB // width
     zcopies = [
-        pltpu.make_async_copy(noise_h, nz.at[:, :, :, pl.ds(LANES, NZ)], noise_sem.at[0]),
-        pltpu.make_async_copy(noise_h.at[:, :, :, pl.ds(NZ - LANES, LANES)], nz.at[:, :, :, pl.ds(0, LANES)], noise_sem.at[1]),
-        pltpu.make_async_copy(noise_h.at[:, :, :, pl.ds(0, LANES)], nz.at[:, :, :, pl.ds(LANES + NZ, LANES)], noise_sem.at[2]),
+        pltpu.make_async_copy(noise_h.at[:, :, :, pl.ds(b * ZB, ZB)], nz.at[b], noise_sem.at[b])
+        for b in range(blocks)
     ]
     for copy in zcopies:
         copy.start()
@@ -102,7 +103,7 @@
     pl.when(has_low)(lambda: greet(g * S - 1))
     pl.when(has_high)(lambda: greet(g * S + S))
 
-    wz[...] = banded(iota(wz.shape, 1) - iota(wz.shape, 0) - LANES, None)
+    wz[...] = banded(iota(wz.shape, 1) - iota(wz.shape, 0) + ROWS, None)
 
     @pl.when(is_edge)
     def _():
@@ -116,31 +117,38 @@
                 hit = jnp.logical_and(col == want + e * half, inside)
                 sel[e, pl.ds(i * LANES, LANES), :] = jnp.where(hit, 1.0, 0.0).astype(BF16)
 
-    for copy in zcopies:
-        copy.wait()
+    def put(b, d, k, c, value):
+        for ph in range(halves):
+            sent[k * comps + c, b * per + d, pl.ds(ph * ROWS, ROWS), :] = (
+                value[:, ph * LANES:(ph + 1) * LANES].astype(BF16)
+            )
+
+    last = ZB - ROWS
+    for group in range(0, blocks, GROUP):
+        these = range(group, min(group + GROUP, blocks))
+        for b in these:
+            zcopies[b].wait()
+        for b in these:
+            for c in range(comps):
+                rhs = nz[b, :, c].reshape(planes * band, ZB)
+                out = lax.dot_general(wz[...], rhs, (((1,), (1,)), ((), ())), preferred_element_type=F32)
+                rim[b, c, 0] = out[:ROWS]
+                rim[b, c, 1] = out[ROWS:2 * ROWS]
+                rim[b, c, 2] = out[ROWS + last:ROWS + ZB]
+                rim[b, c, 3] = out[ROWS + ZB:]
+                for n in range(1, ZB // ROWS - 1):
+                    put(b, n // chunks, n % chunks, c, out[(n + 1) * ROWS:(n + 2) * ROWS])
     for copy in others:
         copy.start()
-
-    per = ZB // width
-
-    def span_block(b, _):
-        first = pl.multiple_of(b * ZB, ZB)
+    for b in range(blocks):
         for c in range(comps):
-            rhs = nz[:, c, :, pl.ds(first, 2 * ZB)].reshape(planes * band, 2 * ZB)
-            out = lax.dot_general(wz[...], rhs, (((1,), (1,)), ((), ())), preferred_element_type=F32)
-            out = out.astype(BF16)
-            for ph in range(halves):
-                part = out[:, ph * LANES:(ph + 1) * LANES].reshape(per, chunks, ROWS, LANES)
-                for k in range(chunks):
-                    sent[k * comps + c, pl.ds(b * per, per), pl.ds(ph * ROWS, ROWS), :] = part[:, k]
-        return 0
-
-    lax.fori_loop(0, NZ // ZB, span_block, 0)
+            put(b, 0, 0, c, rim[b, c, 1] + rim[(b - 1) % blocks, c, 3])
+            put(b, per - 1, chunks - 1, c, rim[b, c, 2] + rim[(b + 1) % blocks, c, 0])
 
     tx, ty, tc = lax.div(t, dims[1] * dims[2]), lax.rem(lax.div(t, dims[2]), dims[1]), lax.rem(t, dims[2])
 
     def dest_tile(j):
-        dx, dy, dc = lax.div(j, dims[1] * dims[2]), lax.rem(lax.div(j, dims[2]), dims[1]), lax.rem(j, dims[2])
+        dy, dx, dc = lax.div(j, dims[0] * dims[2]), lax.rem(lax.div(j, dims[2]), dims[0]), lax.rem(j, dims[2])
         return (lax.rem(tx + dx, dims[0]) * dims[1] + lax.rem(ty + dy, dims[1])) * dims[2] + lax.rem(tc + dc, dims[2])
 
     @pl.when(is_edge)
@@ -369,7 +377,7 @@
     cuts = chunks * comps
     hbm_spec = pl.BlockSpec(memory_space=pltpu.HBM)
     vmem_spec = pl.BlockSpec(memory_space=pltpu.VMEM)
-    return pl.pallas_call(
+    inflow, out = pl.pallas_call(
         functools.partial(kernel, cfg),
         out_shape=(
             pltpu.VMEM((planes * G, comps, width, length), BF16),
@@ -378,14 +386,15 @@
         in_specs=[hbm_spec] * 7,
         out_specs=(vmem_spec, vmem_spec),
         scratch_shapes=[
-            pltpu.VMEM((planes, comps, band, NZ + 2 * LANES), BF16),
+            pltpu.VMEM((NZ // ZB, planes, comps, band, ZB), BF16),
             pltpu.VMEM(stress.shape, F32),
             pltpu.VMEM(timescale.shape, F32),
             pltpu.VMEM(mean_inflow.shape, F32),
             pltpu.VMEM(courant.shape, F32),
             pltpu.VMEM(prior_state.shape, F32),
             pltpu.VMEM(field.shape, F32),
-            pltpu.VMEM((ZB, 2 * ZB), BF16),
+            pltpu.VMEM((NZ // ZB, comps, 4, ROWS, planes * band), F32),
+            pltpu.VMEM((ZB + 2 * ROWS, ZB), BF16),
             pltpu.VMEM((4 * LANES, 2 * LANES), BF16),
             pltpu.VMEM((2, pairs * LANES, LANES), BF16),
             pltpu.VMEM((2, 2, LANES, pairs * LANES), BF16),
@@ -395,7 +404,7 @@
             pltpu.VMEM((2, G, chunks // 2 * ROWS, LANES), BF16),
             pltpu.VMEM((length // LANES, G * halves * ROWS, 2 * LANES), F32),
             pltpu.VMEM((comps - 1, length // LANES, planes * G, ROWS, LANES), F32),
-            pltpu.SemaphoreType.DMA((3,)),
+            pltpu.SemaphoreType.DMA((NZ // ZB,)),
             pltpu.SemaphoreType.DMA((6,)),
             pltpu.SemaphoreType.DMA((cuts,)),
             pltpu.SemaphoreType.DMA((cuts,)),
@@ -410,6 +419,37 @@
         pltpu.with_memory_space_constraint(v, pltpu.HBM)
         for v in (noise, stress, timescale, mean_inflow, courant, prior_state, field)
     ])
+    return flush(inflow, out)
+
+
+def flush_kernel(inflow_v, out_v, inflow_h, out_h, sems):
+    copies = [
+        pltpu.make_async_copy(inflow_v.at[pl.ds(i * n, n)], inflow_h.at[pl.ds(i * n, n)], sems.at[i])
+        for n in (inflow_h.shape[0] // 4,)
+        for i in range(4)
+    ] + [
+        pltpu.make_async_copy(out_v.at[c], out_h.at[c], sems.at[4 + c]) for c in range(out_h.shape[0])
+    ]
+    for copy in copies:
+        copy.start()
+    for copy in copies:
+        copy.wait()
+
+
+def flush(inflow, out):
+    any_spec = pl.BlockSpec(memory_space=pl.ANY)
+    return pl.pallas_call(
+        flush_kernel,
+        out_shape=(
+            jax.ShapeDtypeStruct(inflow.shape, inflow.dtype),
+            jax.ShapeDtypeStruct(out.shape, out.dtype),
+        ),
+        in_specs=[any_spec] * 2,
+        out_specs=(any_spec, any_spec),
+        scratch_shapes=[pltpu.SemaphoreType.DMA((4 + out.shape[0],))],
+        compiler_params=pltpu.CompilerParams(vmem_limit_bytes=40 * 2**20),
+        name="flush",
+    )(inflow, out)
 
 
 TILE_DIMS = {32: (4, 4, 2), 8: (2, 2, 2), 4: (2, 1, 2)}

time: 54.1 us -> 51 us (0.943)
  local copies, waits for them, and re-layouts: 3.33 us -> 0 us
    unnamed x2 -> x0, local copies, waits for them, and re-layouts: 3.33 us -> none
    pallas_call x1, Pallas kernels: 50.1 us -> 47.1 us  [body(): pl.pallas_call(functools.partial(kernel, cfg), out_shape=(pltpu.VMEM((pla...]
    pallas_call x0 -> x1, Pallas kernels: none -> 2.73 us  [flush(): pl.pallas_call(flush_kernel, out_shape=(jax.ShapeDtypeStruct(inflow.shape...]
where the time goes in v3:
time: 51 us; the launch traced here: 50.5 us
  Pallas kernels  49.9 us (98%)
  between operations  0.64 us (1%)
    pallas_call x1, Pallas kernels, body(): pl.pallas_call(functools.partial(kernel, cfg), out_shape=(pltpu.VMEM((pla...  47.1 us
    pallas_call x1, Pallas kernels, flush(): pl.pallas_call(flush_kernel, out_shape=(jax.ShapeDtypeStruct(inflow.shape...  2.73 us

profile of v3, /device:TPU:5, one launch (start us, length us, event | category | flops | bytes accessed | tf_op | source)
XLA Modules:
  0.0 50.5 jit_solution(4435995843908967410)
XLA Ops:
  0.6 47.1 %inflow.1 = (bf16[16,3,64,512]{3,2,1,0:T(8,128)(2,1)S(1)}, f32[3,8,64,512]{3,2,1,0:T(8,128)S(1)}) custom-call(bf16[4,3,64,2048]{3,2,1,0:T(8,128)(2,1)} %noise_h.1, f32[6,64,512]{2,1,0:T(8,128)} %stress_h.1, f32[64,512]{1,0:T(8,128)} %time_h.1, f32[64,512]{1,0:T(8,128)} %mean_h.1, f32[64,512]{1,0:T(8,128)} %courant_h.1, f32[3,64,512]{2,1,0:T(8,128)} %prior_h.1, ...), custom_call_target="tpu_custom_call" | custom-call | tf_op jit(solution)/shard_map/inflow/pallas_call | solution.py:380
  47.8 2.7 %flush.1 = (bf16[16,3,64,512]{3,2,1,0:T(8,128)(2,1)}, f32[3,8,64,512]{3,2,1,0:T(8,128)}) custom-call(bf16[16,3,64,512]{3,2,1,0:T(8,128)(2,1)S(1)} %get-tuple-element.4.inflow_v, f32[3,8,64,512]{3,2,1,0:T(8,128)S(1)} %get-tuple-element.5.out_v), custom_call_target="tpu_custom_call" | custom-call | tf_op jit(solution)/shard_map/flush/pallas_call | solution.py:441

commit v4 on v3

--- a/solution.py
+++ b/solution.py
@@ -203,16 +203,7 @@
 
         return lax.fori_loop(first_send, TN, send, 0)
 
-    lax.fori_loop(0, chunks * comps, send_chunk, 0)
-
-    @pl.when(is_self)
-    def _():
-        got[:, my_slot] = sent[:, t]
-
-    @pl.when(own_halo)
-    def _():
-        side = jnp.where(edge_high, none, one)
-        got_halo[side, g] = sent_halo[t]
+    send_chunk(0, 0)
 
     row, col = iota(wy.shape, 0), iota(wy.shape, 1)
     wy[...] = banded(
@@ -228,6 +219,17 @@
             for e in range(2):
                 hit = jnp.logical_and(row == want + e * half, jnp.logical_and(y >= top, y < top + FW))
                 unsel[side, e, :, pl.ds(i * LANES, LANES)] = jnp.where(hit, 1.0, 0.0).astype(BF16)
+    lax.fori_loop(1, chunks * comps, send_chunk, 0)
+
+    @pl.when(is_self)
+    def _():
+        got[:, my_slot] = sent[:, t]
+
+    @pl.when(own_halo)
+    def _():
+        side = jnp.where(edge_high, none, one)
+        got_halo[side, g] = sent_halo[t]
+
     for copy in others:
         copy.wait()
 

time: 51 us -> 50.8 us (level)
  no operation moved by 1% of the time
where the time goes in v4:
time: 50.8 us; the launch traced here: 50.5 us
  Pallas kernels  49.9 us (98%)
  between operations  0.64 us (1%)
    pallas_call x1, Pallas kernels, body(): pl.pallas_call(functools.partial(kernel, cfg), out_shape=(pltpu.VMEM((pla...  47.1 us
    pallas_call x1, Pallas kernels, flush(): pl.pallas_call(flush_kernel, out_shape=(jax.ShapeDtypeStruct(inflow.shape...  2.73 us

profile of v4, /device:TPU:5, one launch (start us, length us, event | category | flops | bytes accessed | tf_op | source)
XLA Modules:
  0.0 50.5 jit_solution(4385236249572170648)
XLA Ops:
  0.6 47.1 %inflow.1 = (bf16[16,3,64,512]{3,2,1,0:T(8,128)(2,1)S(1)}, f32[3,8,64,512]{3,2,1,0:T(8,128)S(1)}) custom-call(bf16[4,3,64,2048]{3,2,1,0:T(8,128)(2,1)} %noise_h.1, f32[6,64,512]{2,1,0:T(8,128)} %stress_h.1, f32[64,512]{1,0:T(8,128)} %time_h.1, f32[64,512]{1,0:T(8,128)} %mean_h.1, f32[64,512]{1,0:T(8,128)} %courant_h.1, f32[3,64,512]{2,1,0:T(8,128)} %prior_h.1, ...), custom_call_target="tpu_custom_call" | custom-call | tf_op jit(solution)/shard_map/inflow/pallas_call | solution.py:382
  47.8 2.7 %flush.1 = (bf16[16,3,64,512]{3,2,1,0:T(8,128)(2,1)}, f32[3,8,64,512]{3,2,1,0:T(8,128)}) custom-call(bf16[16,3,64,512]{3,2,1,0:T(8,128)(2,1)S(1)} %get-tuple-element.4.inflow_v, f32[3,8,64,512]{3,2,1,0:T(8,128)S(1)} %get-tuple-element.5.out_v), custom_call_target="tpu_custom_call" | custom-call | tf_op jit(solution)/shard_map/flush/pallas_call | solution.py:443
